TPU v7x, 32 devices: a whole 2x2x4 slice. The times are simulated.
32 devices in a mesh: pipe: 2 (over x), tensor: 2 (over core), dp: 8 (over z, y).
Axes of the slice: x: 2, y: 2, z: 4, core: 2. Of those that a mesh axis runs over, the one named last changes fastest.
Arguments:
- attn_out: bfloat16 [2, 4, 1024, 4096], P('pipe', None, 'dp', 'tensor'), may hold values from -6 to 6
- grad_top: bfloat16 [4, 1024, 4096], P(None, 'dp', 'tensor'), may hold values from -6 to 6
- branch_grad: bfloat16 [2, 4, 1024, 4096], P('pipe', None, 'dp', 'tensor'), may hold values from -6 to 6
- error_prev: bfloat16 [2, 8, 4096, 4096], P('pipe', 'dp', 'tensor'), may hold values from -0.3984375 to 0.3984375
- q_prev: float32 [2, 4096, 64], P('pipe', 'tensor'), may hold values from -6 to 6
Outputs:
- grad_input: bfloat16 [2, 4, 1024, 4096], P('pipe', None, 'dp', 'tensor')
- error_next: bfloat16 [2, 8, 4096, 4096], P('pipe', 'dp', 'tensor')
- p_factor: float32 [2, 4096, 64], P('pipe', 'tensor')
- q_factor: float32 [2, 4096, 64], P('pipe', 'tensor')
All inputs are finite; a program needn't handle non-finite values.
Results may differ from a plain program's by a relative error of at most 0.012.
Values may be sent and summed in bfloat16 or wider, within the bound.
A program may use at most 256 MiB of HBM per device.

v0:
```python
import jax
import jax.numpy as jnp
from jax import lax
from jax.sharding import PartitionSpec as P


def from_behind(value, axis, by):
    devices = lax.axis_size(axis)
    pairs = [(i, i + by) for i in range(devices) if 0 <= i + by < devices]
    return lax.ppermute(value, axis, pairs)


def add_round(a, b):
    return (a.astype(jnp.float32) + b.astype(jnp.float32)).astype(jnp.bfloat16)


def two_terms(x):
    head = x.astype(jnp.bfloat16)
    tail = (x - head.astype(jnp.float32)).astype(jnp.bfloat16)
    return head, tail


def sum_of_shares(value, axes):
    count = lax.axis_size(axes)
    rows, cols = value.shape
    pieces = value.astype(jnp.bfloat16).reshape(count, rows // count, cols)
    landed = lax.all_to_all(pieces, axes, split_axis=0, concat_axis=0, tiled=True)
    return jnp.sum(landed.astype(jnp.float32), axis=0)


def on_device(attn_out, grad_top, branch_grad, error_prev, q_prev):
    high = lax.Precision.HIGHEST
    section = lax.axis_index("pipe")
    sections = lax.axis_size("pipe")
    last = sections - 1
    micro_count, tok_rows, features = grad_top.shape
    head_rows = attn_out.shape[3]
    replicas = lax.axis_size("dp")
    tokens = micro_count * tok_rows
    branch = branch_grad[0]

    out_grads, grad_ins = [], []
    for micro in range(micro_count):
        out = grad_top[micro]
        for hop in range(sections - 1):
            if hop == 0:
                back = add_round(grad_top[micro], from_behind(branch[micro], "pipe", -1))
            else:
                back = from_behind(add_round(out, branch[micro]), "pipe", -1)
            out = jnp.where(section == last, grad_top[micro], back)
        out_grads.append(out)
        grad_ins.append(add_round(out, branch[micro]))
    grad_all = jnp.stack(grad_ins)
    out_all = lax.all_gather(jnp.concatenate(out_grads, axis=0), "tensor", axis=1, tiled=True)
    grads = lax.dot_general(
        attn_out[0].reshape(tokens, head_rows),
        out_all,
        (((0,), (0,)), ((), ())),
        preferred_element_type=jnp.float32,
    )
    matrix = (grads / tokens + error_prev[0, 0].astype(jnp.float32)).astype(jnp.bfloat16)

    rank = q_prev.shape[2]
    q_old = lax.all_gather(q_prev[0], "tensor", axis=0, tiled=True)
    p_two = jnp.dot(
        matrix, jnp.concatenate(two_terms(q_old), axis=1), preferred_element_type=jnp.float32
    )
    p_local = p_two[:, :rank] + p_two[:, rank:]
    p_rows = sum_of_shares(p_local, "dp") / replicas
    praw = lax.all_gather(p_rows, "dp", axis=0, tiled=True)
    gram = lax.psum(jnp.dot(praw.T, praw, precision=high), "tensor")
    lower = jnp.linalg.cholesky(gram)
    phat = lax.linalg.triangular_solve(lower, praw, left_side=False, lower=True, transpose_a=True)
    p_terms = jnp.concatenate(two_terms(phat), axis=1)
    q_two = lax.dot_general(
        matrix, p_terms, (((0,), (0,)), ((), ())), preferred_element_type=jnp.float32
    )
    q_local = q_two[:, :rank] + q_two[:, rank:]
    q_rows = sum_of_shares(q_local, ("tensor", "dp")) / replicas
    q_full = lax.all_gather(q_rows.astype(jnp.bfloat16), ("tensor", "dp"), axis=0, tiled=True)
    own = q_prev.shape[1]
    q_own = lax.dynamic_slice_in_dim(q_full, lax.axis_index("tensor") * own, own, 0)
    low_rank = lax.dot_general(
        p_terms,
        jnp.concatenate([q_full, q_full], axis=1),
        (((1,), (1,)), ((), ())),
        preferred_element_type=jnp.float32,
    )
    error_next = (matrix.astype(jnp.float32) - low_rank).astype(jnp.bfloat16)
    return (grad_all[None], error_next[None, None], phat[None], q_own.astype(jnp.float32)[None])


def solution(mesh):
    return jax.shard_map(
        on_device,
        mesh=mesh,
        in_specs=(
            P("pipe", None, "dp", "tensor"),
            P(None, "dp", "tensor"),
            P("pipe", None, "dp", "tensor"),
            P("pipe", "dp", "tensor", None),
            P("pipe", "tensor", None),
        ),
        out_specs=(
            P("pipe", None, "dp", "tensor"),
            P("pipe", "dp", "tensor", None),
            P("pipe", "tensor", None),
            P("pipe", "tensor", None),
        ),
        check_vma=False,
    )
```

profile of v0, /device:TPU:1, one launch (start us, length us, event | category | flops | bytes accessed | tf_op | source)
XLA Modules:
  0.0 285.6 jit_solution(16449809719552677688)
XLA Ops:
  7.2 0.0 copy-start
  7.2 0.0 all-gather.6.cloned.1.call-start
  7.2 2.8 slice_bitcast_fusion.3
  10.0 1.3 collective-permute-start
  11.3 1.3 collective-permute-start.1
  12.6 1.3 collective-permute-start.3
  13.9 1.3 collective-permute-start.2
  15.2 0.0 all-gather.6.cloned.1.call-update
  15.3 0.0 all-gather.4.cloned.1.call-start
  15.3 10.1 %collective-permute-done = bf16[128,2048]{1,0:T(8,128)(2,1)} collective-permute-done((bf16[128,2048]{1,0:T(8,128)(2,1)}, bf16[128,2048]{1,0:T(8,128)(2,1)}, u32[]{:S(2)}, u32[]{:S(2)}) %collective-permute-start) | collective-permute-done | bytes 524320 | tf_op jit(solution)/shard_map/ppermute | solution.py:10
  25.4 11.2 %collective-permute-done.1 = bf16[128,2048]{1,0:T(8,128)(2,1)} collective-permute-done((bf16[128,2048]{1,0:T(8,128)(2,1)}, bf16[128,2048]{1,0:T(8,128)(2,1)}, u32[]{:S(2)}, u32[]{:S(2)}) %collective-permute-start.1) | collective-permute-done | bytes 524320 | tf_op jit(solution)/shard_map/ppermute | solution.py:10
  36.6 11.2 %collective-permute-done.3 = bf16[128,2048]{1,0:T(8,128)(2,1)} collective-permute-done((bf16[128,2048]{1,0:T(8,128)(2,1)S(1)}, bf16[128,2048]{1,0:T(8,128)(2,1)}, u32[]{:S(2)}, u32[]{:S(2)}) %collective-permute-start.3) | collective-permute-done | bytes 524320 | tf_op jit(solution)/shard_map/ppermute | solution.py:10
  47.8 11.2 %collective-permute-done.2 = bf16[128,2048]{1,0:T(8,128)(2,1)} collective-permute-done((bf16[128,2048]{1,0:T(8,128)(2,1)S(1)}, bf16[128,2048]{1,0:T(8,128)(2,1)}, u32[]{:S(2)}, u32[]{:S(2)}) %collective-permute-start.2) | collective-permute-done | bytes 524320 | tf_op jit(solution)/shard_map/ppermute | solution.py:10
  59.1 5.3 %fusion.15 = (bf16[1,128,2048]{2,1,0:T(8,128)(2,1)}, bf16[128,2048]{1,0:T(8,128)(2,1)S(1)}, bf16[1,128,2048]{2,1,0:T(8,128)(2,1)}, bf16[128,2048]{1,0:T(8,128)(2...) fusion(bf16[1,4,128,2048]{3,2,1,0:T(8,128)(2,1)} %param.7, ...), kind=kLoop, calls=%fused_computation.31 | loop fusion | flops 9437184 | bytes 10485761 | tf_op jit(solution)/shard_map/stack | solution.py:53
  64.4 1.6 pad_maximum_fusion
  66.0 0.0 all-gather.4.cloned.1.call-update
  66.0 22.0 %copy.14 = bf16[1,1,2048,4096]{2,3,1,0:T(8,128)(2,1)} copy(bf16[1,1,2048,4096]{3,2,1,0:T(8,128)(2,1)} %param.8) | data formatting | bytes 33554432 | tf_op args[3]
  87.9 0.0 all-gather.6.cloned.1.call-done
  87.9 1.3 fusion.10
  89.3 0.0 all-gather.4.cloned.1.call-done
  89.3 0.0 copy-done
  89.3 18.0 %fusion = bf16[2048,4096]{0,1:T(8,128)(2,1)} fusion(bf16[512,4096]{1,0:T(8,128)(2,1)} %all-gather.4.cloned.1.call-done, bf16[512,2048]{1,0:T(8,128)(2,1)S(1)} %bitcast.82, bf16[1,1,2048,4096]{2,3,1,0:T(8,128)(2,1)} %copy.14), kind=kOutput, calls=%fused_computation.1 | convolution fusion | flops 8623489024 | bytes 39845888 | tf_op jit(solution)/shard_map/dot_general | solution.py:55
  107.3 8.1 %fusion.3 = f32[2048,128]{0,1:T(8,128)S(1)} fusion(bf16[2048,4096]{0,1:T(8,128)(2,1)} %fusion, bf16[4096,64]{0,1:T(8,128)(2,1)S(1)} %get-tuple-element.12, bf16[4096,64]{0,1:T(8,128)(2,1)S(1)} %get-tuple-element.13), kind=kOutput, calls=%fused_computation.8 | convolution fusion | flops 2149580800 | bytes 18874368 | tf_op jit(solution)/shard_map/dot_general | solution.py:65
  115.5 0.1 fusion.19
  115.5 14.0 %all_to_all.10 = bf16[8,256,64]{1,2,0:T(8,128)(2,1)S(1)} all-to-all(bf16[8,256,64]{1,2,0:T(8,128)(2,1)S(1)} %bitcast.85), channel_id=1, replica_groups=mesh['pipe'=2,'tensor'=2,'dp'=8] {'dp'}, dimensions={0} | all-to-all | bytes 524288 | tf_op jit(solution)/shard_map/all_to_all | solution.py:27
  129.6 25.6 %all_gather.14 = f32[2048,64]{0,1:T(8,128)S(1)} all-gather(f32[256,64]{0,1:T(8,128)S(1)} %broadcast_multiply_fusion), channel_id=1, replica_groups=mesh['pipe'=2,'tensor'=2,'dp'=8] {'dp'}, dimensions={0}, use_global_device_ids=true | all-gather | bytes 589824 | tf_op jit(solution)/shard_map/all_gather | solution.py:70
  155.2 0.6 fusion.33
  155.8 11.8 %psum.7 = f32[64,64]{0,1:T(8,128)S(1)} all-reduce(f32[64,64]{0,1:T(8,128)S(1)} %fusion.33), channel_id=1, replica_groups=mesh['pipe'=2,'tensor'=2,'dp'=8] {'tensor'}, use_global_device_ids=true, to_apply=%region_1.2 | all-reduce | flops 4096 | bytes 32768 | tf_op jit(solution)/shard_map/psum | solution.py:71
  167.6 0.1 copy.17
  167.7 5.8 %cholesky.16 = f32[64,64]{1,0:T(8,128)S(1)} custom-call(f32[64,64]{1,0:T(8,128)S(1)} %fusion.24), custom_call_target="Cholesky" | custom-call | tf_op jit(solution)/shard_map/jit(cholesky)/cholesky | solution.py:72
  173.6 0.6 compare_reduce_fusion
  174.2 0.7 fusion.21
  174.9 4.9 %custom-call.6 = f32[1,64,64]{1,2,0:T(8,128)S(1)} custom-call(f32[1,64,64]{2,1,0:T(8,128)S(1)} %fusion.21), custom_call_target="InvertDiagBlocksLowerTriangular" | custom-call | tf_op jit(solution)/shard_map/triangular_solve | solution.py:73
  179.8 1.4 fusion.32
  181.2 0.0 copy-start.4
  181.2 11.5 %fusion.20 = f32[4096,128]{0,1:T(8,128)S(1)} fusion(bf16[2048,4096]{0,1:T(8,128)(2,1)} %fusion, bf16[2048,64]{0,1:T(8,128)(2,1)S(1)} %get-tuple-element.33, bf16[2048,64]{0,1:T(8,128)(2,1)S(1)} %get-tuple-element.32), kind=kOutput, calls=%fused_computation.45 | convolution fusion | flops 2148532224 | bytes 19398656 | tf_op jit(solution)/shard_map/dot_general | solution.py:75
  192.7 0.0 copy-done.4
  192.7 0.0 copy-start.2
  192.7 0.0 copy-start.3
  192.7 0.1 fusion.2
  192.8 0.0 copy-start.5
  192.8 0.8 copy.27
  193.7 3.6 %all-to-all-start.1 = ((bf16[16,256,64]{1,2,0:T(8,128)(2,1)}), bf16[16,256,64]{1,2,0:T(8,128)(2,1)S(1)}, u32[]{:S(2)}, u32[]{:S(2)}) async-start(bf16[16,256,64]{1,2,0:T(8,128)(2,1)} %bitcast.80), calls=%async_computation.1 | async-start | bytes 1048576 | tf_op jit(solution)/shard_map/all_to_all | solution.py:27
  197.2 0.0 copy-done.2
  197.3 0.0 copy-done.3
  197.3 2.8 maximum_bitcast_fusion
  200.0 11.5 %all-to-all-done.1 = bf16[16,256,64]{1,2,0:T(8,128)(2,1)S(1)} async-done(((bf16[16,256,64]{1,2,0:T(8,128)(2,1)}), bf16[16,256,64]{1,2,0:T(8,128)(2,1)S(1)}, u32[]{:S(2)}, u32[]{:S(2)}) %all-to-all-start.1) | async-done | bytes 524320 | tf_op jit(solution)/shard_map/all_to_all | solution.py:27
  211.6 0.1 convert_reduce_fusion
  211.7 33.4 %all_gather.15 = bf16[4096,64]{0,1:T(8,128)(2,1)S(1)} all-gather(bf16[256,64]{0,1:T(8,128)(2,1)S(1)} %multiply_convert_fusion), channel_id=1, replica_groups=mesh['pipe'=2,'tensor'=2,'dp'=8] {'tensor','dp'}, dimensions={0}, use_global_device_ids=true | all-gather | bytes 557056 | tf_op jit(solution)/shard_map/all_gather | solution.py:80
  245.1 0.0 copy-done.5
  245.1 11.5 %fusion.1 = bf16[1,1,2048,4096]{2,3,1,0:T(8,128)(2,1)} fusion(bf16[2048,4096]{0,1:T(8,128)(2,1)} %fusion, bf16[4096,64]{0,1:T(8,128)(2,1)S(1)} %all_gather.15, bf16[2048,64]{0,1:T(8,128)(2,1)S(1)} %copy-done.5, bf16[2048,64]{0,1:T(8,128)(2,1)S(1)} %get-tuple-element.32), kind=kOutput, calls=%fused_computation.3 | convolution fusion | flops 2175795200 | bytes 34603008 | tf_op jit(solution)/shard_map/dot_general | solution.py:83
  256.6 0.8 bitcast_convert_fusion.1
  257.4 0.0 copy-start.1
  257.4 21.3 %copy.20 = bf16[1,1,2048,4096]{3,2,1,0:T(8,128)(2,1)} copy(bf16[1,1,2048,4096]{2,3,1,0:T(8,128)(2,1)} %fusion.1) | data formatting | bytes 33554432
  278.7 0.0 copy-done.1
  (6 shorter events, 0.1 us)
Async XLA Ops:
  7.2 82.2 %copy-start = (bf16[1,4,128,2048]{3,2,1,0:T(8,128)(2,1)S(1)}, bf16[1,4,128,2048]{3,2,1,0:T(8,128)(2,1)}, u32[]{:S(2)}) copy-start(bf16[1,4,128,2048]{3,2,1,0:T(8,128)(2,1)} %param.5) | copy-start | bytes 6291460
  7.2 80.8 %all-gather.6.cloned.1.call-start = ((), (), s32[]{:S(2)}) async-start(), calls=%async_computation.3 | async-start | bytes 1572864 | tf_op jit(solution)/shard_map/all_gather | solution.py:64
  10.0 15.3 %collective-permute-start = (bf16[128,2048]{1,0:T(8,128)(2,1)}, bf16[128,2048]{1,0:T(8,128)(2,1)}, u32[]{:S(2)}, u32[]{:S(2)}) collective-permute-start(bf16[128,2048]{1,0:T(8,128)(2,1)} %get-tuple-element.28), channel_id=1, source_target_pairs={{16,0},{17,1},{18,2},{19,3},{20,4},{21,5},{22,6},{23,7},{24,8},{25... | collective-permute-start | bytes 1572872 | tf_op jit(solution)/shard_map/ppermute | solution.py:10
  11.3 25.3 %collective-permute-start.1 = (bf16[128,2048]{1,0:T(8,128)(2,1)}, bf16[128,2048]{1,0:T(8,128)(2,1)}, u32[]{:S(2)}, u32[]{:S(2)}) collective-permute-start(bf16[128,2048]{1,0:T(8,128)(2,1)} %get-tuple-element.29), channel_id=1, source_target_pairs={{16,0},{17,1},{18,2},{19,3},{20,4},{21,5},{22,6},{23,7},{24,8},{25... | collective-permute-start | bytes 1572872 | tf_op jit(solution)/shard_map/ppermute | solution.py:10
  12.6 35.2 %collective-permute-start.3 = (bf16[128,2048]{1,0:T(8,128)(2,1)S(1)}, bf16[128,2048]{1,0:T(8,128)(2,1)}, u32[]{:S(2)}, u32[]{:S(2)}) collective-permute-start(bf16[128,2048]{1,0:T(8,128)(2,1)S(1)} %get-tuple-element.30), channel_id=1, source_target_pairs={{16,0},{17,1},{18,2},{19,3},{20,4},{21,5},{22,6},{23,7},{24,8},{25... | collective-permute-start | bytes 1572872 | tf_op jit(solution)/shard_map/ppermute | solution.py:10
  13.9 45.2 %collective-permute-start.2 = (bf16[128,2048]{1,0:T(8,128)(2,1)S(1)}, bf16[128,2048]{1,0:T(8,128)(2,1)}, u32[]{:S(2)}, u32[]{:S(2)}) collective-permute-start(bf16[128,2048]{1,0:T(8,128)(2,1)S(1)} %get-tuple-element.31), channel_id=1, source_target_pairs={{16,0},{17,1},{18,2},{19,3},{20,4},{21,5},{22,6},{23,7},{24,8},{25... | collective-permute-start | bytes 1572872 | tf_op jit(solution)/shard_map/ppermute | solution.py:10
  15.3 74.1 %all-gather.4.cloned.1.call-start = ((), (), s32[]{:S(2)}) async-start(), calls=%async_computation.2 | async-start | bytes 6291456 | tf_op jit(solution)/shard_map/all_gather | solution.py:54
  181.2 11.5 %copy-start.4 = (bf16[2048,64]{0,1:T(8,128)(2,1)}, bf16[2048,64]{0,1:T(8,128)(2,1)S(1)}, u32[]{:S(2)}) copy-start(bf16[2048,64]{0,1:T(8,128)(2,1)S(1)} %get-tuple-element.33) | copy-start | bytes 786436
  192.7 4.6 %copy-start.2 = (bf16[1,128,2048]{2,1,0:T(8,128)(2,1)S(1)}, bf16[1,128,2048]{2,1,0:T(8,128)(2,1)}, u32[]{:S(2)}) copy-start(bf16[1,128,2048]{2,1,0:T(8,128)(2,1)} %get-tuple-element.14) | copy-start | bytes 1572868
  192.7 4.6 %copy-start.3 = (bf16[1,128,2048]{2,1,0:T(8,128)(2,1)S(1)}, bf16[1,128,2048]{2,1,0:T(8,128)(2,1)}, u32[]{:S(2)}) copy-start(bf16[1,128,2048]{2,1,0:T(8,128)(2,1)} %get-tuple-element.22) | copy-start | bytes 1572868
  192.8 52.3 %copy-start.5 = (bf16[2048,64]{0,1:T(8,128)(2,1)S(1)}, bf16[2048,64]{0,1:T(8,128)(2,1)}, u32[]{:S(2)}) copy-start(bf16[2048,64]{0,1:T(8,128)(2,1)} %copy-done.4) | copy-start | bytes 786436
  193.7 17.9 %all-to-all-start.1 = ((bf16[16,256,64]{1,2,0:T(8,128)(2,1)}), bf16[16,256,64]{1,2,0:T(8,128)(2,1)S(1)}, u32[]{:S(2)}, u32[]{:S(2)}) async-start(bf16[16,256,64]{1,2,0:T(8,128)(2,1)} %bitcast.80), calls=%async_computation.1 | async-start | bytes 1048576 | tf_op jit(solution)/shard_map/all_to_all | solution.py:27
  257.4 21.3 %copy-start.1 = (bf16[1,4,128,2048]{3,2,1,0:T(8,128)(2,1)S(1)}, bf16[1,4,128,2048]{3,2,1,0:T(8,128)(2,1)}, u32[]{:S(2)}) copy-start(bf16[1,4,128,2048]{3,2,1,0:T(8,128)(2,1)} %param.5) | copy-start | bytes 6291460
Sparse Core Ops, SparseCore 0:
  15.4 15.7 all-gather.5
  66.1 15.7 all-gather.3
where the time goes:
time: 287 us; the launch traced here: 286 us
  blocking collectives  84.8 us (30%)
  waiting for transfers between devices  55.4 us (19%)
  matrix products  51.1 us (18%)
  local copies, waits for them, and re-layouts  47.1 us (16%)
  other arithmetic  24.2 us (8%)
  between operations  14.3 us (5%)
  starting transfers between devices  8.82 us (3%)
    ppermute x4, waiting for transfers between devices, from_behind(): return lax.ppermute(value, axis, pairs)  43.8 us
    unnamed x14, local copies, waits for them, and re-layouts  43.3 us
    all_gather x1, blocking collectives, on_device(): lax.all_gather(q_rows.astype(jnp.bfloat16), ('tensor', 'dp'), axis=0, til...  33.4 us
    all_gather x1, blocking collectives, on_device(): praw = lax.all_gather(p_rows, 'dp', axis=0, tiled=True)  25.6 us
    dot_general x1, matrix products, on_device(): lax.dot_general(attn_out[0].reshape(tokens, head_rows), out_all, (((0,),...  18 us
    all_to_all x1, blocking collectives, sum_of_shares(): lax.all_to_all(pieces, axes, split_axis=0, concat_axis=0, tiled=True)  14 us
    psum x1, blocking collectives, on_device(): gram = lax.psum(jnp.dot(praw.T, praw, precision=high), 'tensor')  11.8 us
    all_to_all x1, waiting for transfers between devices, sum_of_shares(): lax.all_to_all(pieces, axes, split_axis=0, concat_axis=0, tiled=True)  11.5 us
  transfers between devices with their start and end apart: 7, of which 5 were waited for; matrix products, arithmetic and copies ran while one was open for 12% of the time, Pallas kernels for 0%

commit v1 on v0

v1 whole, which is shorter than its diff:
```python
import functools

import jax
import jax.numpy as jnp
from jax import lax
from jax.experimental import pallas as pl
from jax.experimental.pallas import tpu as pltpu
from jax.sharding import PartitionSpec as P

BF16 = jnp.bfloat16
F32 = jnp.float32
NN = (((1,), (0,)), ((), ()))
NT = (((1,), (1,)), ((), ()))
TN = (((0,), (0,)), ((), ()))


def mm(a, b, dims):
    return lax.dot_general(a, b, dims, preferred_element_type=F32)


def terms(x):
    head = x.astype(BF16)
    tail = (x - head.astype(F32)).astype(BF16)
    return jnp.concatenate([head, tail], axis=0)


def fold(y):
    half = y.shape[0] // 2
    return y[:half] + y[half:]


def add_round(a, b):
    return (a.astype(F32) + b.astype(F32)).astype(BF16)


def inverse_factor(gram):
    rank = gram.shape[0]
    row = lax.broadcasted_iota(jnp.int32, (rank, 2 * rank), 0)
    col = lax.broadcasted_iota(jnp.int32, (rank, 2 * rank), 1)
    work = jnp.concatenate([gram, jnp.where(row == col, 1.0, 0.0)[:, :rank]], axis=1)
    for k in range(rank - 1):
        ratio = work[:, k : k + 1] * (1.0 / work[k : k + 1, k : k + 1])
        work = work - jnp.where(row > k, ratio * work[k : k + 1, :], 0.0)
    diagonal = jnp.sum(jnp.where(row == col, work, 0.0), axis=1, keepdims=True)
    return work[:, rank:] * lax.rsqrt(diagonal)


class Semaphores:
    def __init__(self):
        self.count = 0

    def take(self, n=1):
        first = self.count
        self.count += n
        return first


def semaphore_map(tensor, dp, bulk, tiles):
    s = Semaphores()
    names = {}
    for name, n in (
        ("err", tiles), ("g_out", 1),
        ("q_s", tensor), ("q_r", tensor), ("q0_s", 1), ("q0_r", 1),
        ("bulk_s", bulk), ("bulk_r", bulk), ("gx_s", 1), ("gx_r", 1),
        ("gq_s", tensor), ("gq_r", tensor), ("p_s", dp), ("p_r", dp),
        ("pg_s", dp), ("pg_r", dp), ("gram_s", tensor), ("gram_r", tensor),
        ("ap_s", tensor), ("ap_r", tensor), ("qx_s", tensor), ("qx_r", tensor),
        ("g_s", tensor), ("g_r", tensor), ("qp_s", dp), ("qp_r", dp),
        ("qg_s", dp), ("qg_r", dp), ("qf_s", tensor * dp), ("qf_r", tensor * dp),
    ):
        names[name] = s.take(n)
    return names, s.count


def chain_kernel(
    dims, attn, gtop, branch, err_hbm, q_in,
    g_out, p_out, q_out, q_own,
    err, qg, q0, gadd, land, gbuf, gqx, gqb, eq, psend, prcv, pg, praw, gb,
    phl, apb, qx, qxr, qsend, qrcv, qf, sem,
):
    tensor, dp, bulk, tiles, names = dims
    tokens, head_rows = attn.shape
    features = gtop.shape[1]
    rank = q_in.shape[0]
    pw, qw = head_rows // dp, features // dp
    section = lax.axis_index("pipe")
    t = lax.axis_index("tensor")
    r = lax.axis_index("dp")
    scale = 1.0 / tokens

    def at(name, index=0):
        return sem.at[names[name] + index]

    def remote(src, dst, send, recv, **where):
        return pltpu.make_async_remote_copy(
            src_ref=src, dst_ref=dst, send_sem=send, recv_sem=recv,
            device_id=where, device_id_type=pl.DeviceIdType.MESH,
        )

    tensor_peers = [lax.rem(t + o, tensor) for o in range(1, tensor)]
    dp_peers = [lax.rem(r + o, dp) for o in range(1, dp)]

    def over_tensor(src, dst, key):
        return [
            remote(src, dst.at[t], at(key + "_s", o), at(key + "_r", t), tensor=peer)
            for o, peer in enumerate(tensor_peers)
        ]

    def from_tensor(dst, key):
        for peer in tensor_peers:
            remote(dst.at[peer], dst.at[peer], at(key + "_s"), at(key + "_r", peer), tensor=peer).wait_recv()

    def over_dp(src_of, dst, key):
        return [
            remote(src_of(peer), dst.at[r], at(key + "_s", o), at(key + "_r", r), dp=peer)
            for o, peer in enumerate(dp_peers)
        ]

    def from_dp(dst, key):
        for peer in dp_peers:
            remote(dst.at[peer], dst.at[peer], at(key + "_s"), at(key + "_r", peer), dp=peer).wait_recv()

    def start(copies):
        for copy in copies:
            copy.start()

    def sent(copies):
        for copy in copies:
            copy.wait_send()

    tile = head_rows // tiles

    def err_copy(i):
        rows = pl.ds(pl.multiple_of(i * tile, tile), tile)
        return pltpu.make_async_copy(err_hbm.at[rows], err.at[rows], at("err", i))

    for i in range(tiles):
        err_copy(i).start()
    qg[t] = terms(q_in[...])

    barrier = pltpu.get_barrier_semaphore()
    for peer in tensor_peers:
        pl.semaphore_signal(barrier, inc=1, device_id={"tensor": peer}, device_id_type=pl.DeviceIdType.MESH)
    for peer in dp_peers:
        pl.semaphore_signal(barrier, inc=1, device_id={"dp": peer}, device_id_type=pl.DeviceIdType.MESH)
    pl.semaphore_signal(barrier, inc=1, device_id={"pipe": 1 - section}, device_id_type=pl.DeviceIdType.MESH)
    pl.semaphore_wait(barrier, tensor + dp - 1)

    q_copies = over_tensor(qg.at[t], qg, "q")
    start(q_copies)
    q0_copy = remote(qg.at[t, pl.ds(0, rank)], q0, at("q0_s"), at("q0_r"), pipe=1 - section)
    gx_copy = remote(gqx, gqb.at[t], at("gx_s"), at("gx_r"), pipe=1 - section)
    piece = tokens // bulk

    def bulk_copy(i):
        rows = pl.ds(i * piece, piece)
        return remote(branch.at[rows], land.at[rows], at("bulk_s", i), at("bulk_r", i), pipe=1 - section)

    @pl.when(section == 0)
    def _():
        q0_copy.start()

    @pl.when(section == 1)
    def _():
        bulk_copy(0).start()
        gadd[...] = add_round(gtop[...], branch[...])
        gqb[t] = fold(mm(qg[t], gtop[...], NT)) * scale

    from_tensor(qg, "q")

    def eq_tile(i, carry):
        err_copy(i).wait()
        rows = pl.ds(pl.multiple_of(i * tile, tile), tile)
        total = mm(qg[0], err[rows, pl.ds(0, features)], NT)
        for tt in range(1, tensor):
            total += mm(qg[tt], err[rows, pl.ds(tt * features, features)], NT)
        eq[:, rows] = fold(total)
        return carry

    lax.fori_loop(0, tiles, eq_tile, 0)

    @pl.when(section == 1)
    def _():
        q0_copy.wait_recv()
        gqx[...] = mm(q0[...], gadd[...], NT) * scale
        gx_copy.start()
        for i in range(1, bulk):
            bulk_copy(i).start()

    @pl.when(section == 0)
    def _():
        gx_copy.wait_recv()

    gq_copies = over_tensor(gqb.at[t], gqb, "gq")
    start(gq_copies)
    from_tensor(gqb, "gq")
    gq = gqb[0]
    for tt in range(1, tensor):
        gq += gqb[tt]
    p_local = (fold(mm(terms(gq), attn[...], NN)) + eq[...]).astype(BF16)
    for j in range(dp):
        psend[j] = p_local[:, j * pw : (j + 1) * pw]
    p_copies = over_dp(lambda peer: psend.at[peer], prcv, "p")
    start(p_copies)
    from_dp(prcv, "p")
    total = psend[r].astype(F32)
    for peer in dp_peers:
        total += prcv[peer].astype(F32)
    pg[r] = (total * (1.0 / dp)).astype(BF16)
    pg_copies = over_dp(lambda peer: pg.at[r], pg, "pg")
    start(pg_copies)
    from_dp(pg, "pg")
    for j in range(dp):
        praw[:, j * pw : (j + 1) * pw] = pg[j]

    gb[t] = mm(praw[...], praw[...], NT)
    gram_copies = over_tensor(gb.at[t], gb, "gram")
    start(gram_copies)
    from_tensor(gb, "gram")
    gram = gb[0]
    for tt in range(1, tensor):
        gram += gb[tt]
    inverse = inverse_factor(gram)
    head = inverse.astype(BF16)
    rest = inverse - head.astype(F32)
    middle = rest.astype(BF16)
    last = (rest - middle.astype(F32)).astype(BF16)
    parts = mm(jnp.concatenate([head, middle, last], axis=0), praw[...], NN)
    p = parts[:rank] + (parts[rank : 2 * rank] + parts[2 * rank :])
    p_out[...] = p
    phl[...] = terms(p)
    apb[t] = fold(mm(phl[...], attn[...], NT)) * scale
    ap_copies = over_tensor(apb.at[t], apb, "ap")
    start(ap_copies)

    step = min(features, 512)

    def project(owner, done):
        def column(i, carry):
            here = pl.ds(pl.multiple_of(i * step, step), step)
            there = pl.ds(pl.multiple_of(owner * features + i * step, step), step)
            done(here, fold(mm(phl[...], err[:, there], NN)))
            return carry

        lax.fori_loop(0, features // step, column, 0)

    qx_copies = []
    for o, peer in enumerate(tensor_peers):
        def keep(here, value, slot=o):
            qx[slot, :, here] = value.astype(BF16)

        project(peer, keep)
        copy = remote(qx.at[o], qxr.at[t], at("qx_s", o), at("qx_r", t), tensor=peer)
        copy.start()
        qx_copies.append(copy)

    @pl.when(section == 0)
    def _():
        for i in range(bulk):
            bulk_copy(i).wait_recv()
        gbuf[t] = add_round(gtop[...], land[...])

    @pl.when(section == 1)
    def _():
        gbuf[t] = gtop[...]

    from_tensor(apb, "ap")
    ap = apb[0]
    for tt in range(1, tensor):
        ap += apb[tt]
    apt = terms(ap)

    def keep_own(here, value):
        eq[:, here] = value + fold(mm(apt, gbuf[t, :, here], NN))

    def own_column(i, carry):
        here = pl.ds(pl.multiple_of(i * step, step), step)
        there = pl.ds(pl.multiple_of(t * features + i * step, step), step)
        keep_own(here, fold(mm(phl[...], err[:, there], NN)))
        return carry

    lax.fori_loop(0, features // step, own_column, 0)
    from_tensor(qxr, "qx")
    q_local = eq[:, :features]
    for peer in tensor_peers:
        q_local += qxr[peer].astype(F32)
    q_local = q_local.astype(BF16)
    for j in range(dp):
        qsend[j] = q_local[:, j * qw : (j + 1) * qw]
    qp_copies = over_dp(lambda peer: qsend.at[peer], qrcv, "qp")
    start(qp_copies)
    g_copies = over_tensor(gbuf.at[t], gbuf, "g")
    start(g_copies)
    from_dp(qrcv, "qp")
    total = qsend[r].astype(F32)
    for peer in dp_peers:
        total += qrcv[peer].astype(F32)
    qf[t, r] = (total * (1.0 / dp)).astype(BF16)
    qg_copies = [
        remote(qf.at[t, r], qf.at[t, r], at("qg_s", o), at("qg_r", r), dp=peer)
        for o, peer in enumerate(dp_peers)
    ]
    start(qg_copies)
    qf_copies = []

    def forward(j):
        for o, peer in enumerate(tensor_peers):
            copy = remote(qf.at[t, j], qf.at[t, j], at("qf_s", o * dp + j), at("qf_r", t * dp + j), tensor=peer)
            copy.start()
            qf_copies.append(copy)

    forward(r)
    from_tensor(gbuf, "g")
    g_copy = pltpu.make_async_copy(gbuf, g_out, at("g_out"))
    g_copy.start()
    for peer in dp_peers:
        remote(qf.at[t, peer], qf.at[t, peer], at("qg_s"), at("qg_r", peer), dp=peer).wait_recv()
        forward(peer)
    for j in range(dp):
        q_own[:, j * qw : (j + 1) * qw] = qf[t, j].astype(F32)
    for peer in tensor_peers:
        for j in range(dp):
            remote(qf.at[peer, j], qf.at[peer, j], at("qf_s"), at("qf_r", peer * dp + j), tensor=peer).wait_recv()
    for tt in range(tensor):
        for j in range(dp):
            first = tt * features + j * qw
            q_out[:, first : first + qw] = qf[tt, j]

    @pl.when(section == 0)
    def _():
        q0_copy.wait_send()

    @pl.when(section == 1)
    def _():
        gx_copy.wait_send()
        for i in range(bulk):
            bulk_copy(i).wait_send()

    for copies in (q_copies, gq_copies, p_copies, pg_copies, gram_copies, ap_copies,
                   qx_copies, qp_copies, g_copies, qg_copies, qf_copies):
        sent(copies)
    g_copy.wait()


def chain(mesh, attn, gtop, branch, err, q_t):
    tensor, dp = mesh.shape["tensor"], mesh.shape["dp"]
    tokens, head_rows = attn.shape
    features = gtop.shape[1]
    rank = q_t.shape[0]
    tiles = max(1, head_rows // max(128, head_rows // 8))
    bulk = 8
    names, count = semaphore_map(tensor, dp, bulk, tiles)
    width = tensor * features
    pw, qw = head_rows // dp, features // dp
    wide = max(head_rows, features)
    vmem = pl.BlockSpec(memory_space=pltpu.VMEM)
    anywhere = pl.BlockSpec(memory_space=pl.ANY)
    return pl.pallas_call(
        functools.partial(chain_kernel, (tensor, dp, bulk, tiles, names)),
        out_shape=(
            jax.ShapeDtypeStruct((tensor, tokens, features), BF16),
            jax.ShapeDtypeStruct((rank, head_rows), F32),
            jax.ShapeDtypeStruct((rank, width), BF16),
            jax.ShapeDtypeStruct((rank, features), F32),
        ),
        in_specs=[vmem, vmem, vmem, anywhere, vmem],
        out_specs=(anywhere, vmem, vmem, vmem),
        scratch_shapes=[
            pltpu.VMEM((head_rows, width), BF16),
            pltpu.VMEM((tensor, 2 * rank, features), BF16),
            pltpu.VMEM((rank, features), BF16),
            pltpu.VMEM((tokens, features), BF16),
            pltpu.VMEM((tokens, features), BF16),
            pltpu.VMEM((tensor, tokens, features), BF16),
            pltpu.VMEM((rank, tokens), F32),
            pltpu.VMEM((tensor, rank, tokens), F32),
            pltpu.VMEM((rank, wide), F32),
            pltpu.VMEM((dp, rank, pw), BF16),
            pltpu.VMEM((dp, rank, pw), BF16),
            pltpu.VMEM((dp, rank, pw), BF16),
            pltpu.VMEM((rank, head_rows), BF16),
            pltpu.VMEM((tensor, rank, rank), F32),
            pltpu.VMEM((2 * rank, head_rows), BF16),
            pltpu.VMEM((tensor, rank, tokens), F32),
            pltpu.VMEM((max(1, tensor - 1), rank, features), BF16),
            pltpu.VMEM((tensor, rank, features), BF16),
            pltpu.VMEM((dp, rank, qw), BF16),
            pltpu.VMEM((dp, rank, qw), BF16),
            pltpu.VMEM((tensor, dp, rank, qw), BF16),
            pltpu.SemaphoreType.DMA((count,)),
        ],
        compiler_params=pltpu.CompilerParams(
            collective_id=0, has_side_effects=True, vmem_limit_bytes=56 * 2**20
        ),
        name="chain",
    )(attn, gtop, branch, err, q_t)


def error_kernel(attn, g, err, p, q, out, pair):
    tensor, tokens, features = g.shape
    scale = 1.0 / tokens

    @pl.when(pl.program_id(0) == 0)
    def _():
        pair[...] = jnp.concatenate([q[...], q[...]], axis=0)

    acts = attn[...].T
    fact = terms(p[...]).T
    step = min(features, 512)
    for tt in range(tensor):
        for c in range(features // step):
            here = slice(c * step, (c + 1) * step)
            there = slice(tt * features + c * step, tt * features + (c + 1) * step)
            matrix = mm(acts, g[tt, :, here], NN) * scale + err[:, there].astype(F32)
            out[:, there] = (matrix - mm(fact, pair[:, there], NN)).astype(BF16)


def error_next(attn, g, err, p, q):
    tensor, tokens, features = g.shape
    head_rows, width = err.shape
    rank = p.shape[0]
    tile = max(128, head_rows // 8)
    return pl.pallas_call(
        error_kernel,
        out_shape=jax.ShapeDtypeStruct((head_rows, width), BF16),
        grid=(head_rows // tile,),
        in_specs=[
            pl.BlockSpec((tokens, tile), lambda i: (0, i)),
            pl.BlockSpec((tensor, tokens, features), lambda i: (0, 0, 0)),
            pl.BlockSpec((tile, width), lambda i: (i, 0)),
            pl.BlockSpec((rank, tile), lambda i: (0, i)),
            pl.BlockSpec((rank, width), lambda i: (0, 0)),
        ],
        out_specs=pl.BlockSpec((tile, width), lambda i: (i, 0)),
        scratch_shapes=[pltpu.VMEM((2 * rank, width), BF16)],
        compiler_params=pltpu.CompilerParams(
            dimension_semantics=("arbitrary",), vmem_limit_bytes=48 * 2**20
        ),
        name="error_next",
    )(attn, g, err, p, q)


def on_device(mesh, attn_out, grad_top, branch_grad, error_prev, q_prev):
    micro, rows, features = grad_top.shape
    tokens = micro * rows
    attn = attn_out.reshape(tokens, attn_out.shape[3])
    gtop = grad_top.reshape(tokens, features)
    branch = branch_grad.reshape(tokens, features)
    err = error_prev[0, 0]
    g, p, q, q_own = chain(mesh, attn, gtop, branch, err, q_prev[0].T)
    own = lax.dynamic_index_in_dim(g, lax.axis_index("tensor"), 0, keepdims=False)
    grad_in = add_round(own, branch).reshape(branch_grad.shape)
    error = error_next(attn, g, err, p, q)
    return grad_in, error[None, None], p.T[None], q_own.T[None]


def solution(mesh):
    assert mesh.shape["pipe"] == 2
    return jax.shard_map(
        functools.partial(on_device, mesh),
        mesh=mesh,
        in_specs=(
            P("pipe", None, "dp", "tensor"),
            P(None, "dp", "tensor"),
            P("pipe", None, "dp", "tensor"),
            P("pipe", "dp", "tensor", None),
            P("pipe", "tensor", None),
        ),
        out_specs=(
            P("pipe", None, "dp", "tensor"),
            P("pipe", "dp", "tensor", None),
            P("pipe", "tensor", None),
            P("pipe", "tensor", None),
        ),
        check_vma=False,
    )
```

time: 287 us -> 111 us (0.39)
  Pallas kernels: 0 us -> 102 us
  blocking collectives: 84.8 us -> 0 us
  waiting for transfers between devices: 55.4 us -> 0 us
  matrix products: 51.1 us -> 0 us
  local copies, waits for them, and re-layouts: 47.1 us -> 5.89 us
  other arithmetic: 24.2 us -> 2.12 us
  between operations: 14.3 us -> 0.67 us
  starting transfers between devices: 8.82 us -> 0 us
    pallas_call x0 -> x2, Pallas kernels: none -> 102 us  [the longest x1 80.7 us: chain(): pl.pallas_call(functools.partial(chain_kernel, (tensor, dp, bulk, tiles,...]
    all_gather x2 -> x0, blocking collectives: 59 us -> none  [the longest x1 33.4 us: on_device(): lax.all_gather(q_rows.astype(jnp.bfloat16), ('tensor', 'dp'), axis=0, til...]
    dot_general x5 -> x0, matrix products: 49.6 us -> none  [the longest x1 18 us: on_device(): lax.dot_general(attn_out[0].reshape(tokens, head_rows), out_all, (((0,),...]
    ppermute x4 -> x0, waiting for transfers between devices: 43.8 us -> none  [from_behind(): return lax.ppermute(value, axis, pairs)]
    unnamed x14, local copies, waits for them, and re-layouts: 43.3 us -> 4.02 us
    another operation x6 -> x0, other arithmetic: 17.4 us -> none  [the longest x3 6.52 us: on_device(): lower = jnp.linalg.cholesky(gram)]
    all_to_all x1 -> x0, blocking collectives: 14 us -> none  [sum_of_shares(): lax.all_to_all(pieces, axes, split_axis=0, concat_axis=0, tiled=True)]
    psum x1 -> x0, blocking collectives: 11.8 us -> none  [on_device(): gram = lax.psum(jnp.dot(praw.T, praw, precision=high), 'tensor')]
  transfers between devices with their start and end apart: 7 -> 0, of which waited for: 5 -> 0; matrix products, arithmetic and copies ran while one was open for 12% -> 0% of each run, Pallas kernels for 0% -> 0%
where the time goes in v1:
time: 111 us; the launch traced here: 110 us
  Pallas kernels  102 us (92%)
  local copies, waits for them, and re-layouts  5.89 us (5%)
  other arithmetic  2.12 us (2%)
    pallas_call x1, Pallas kernels, chain(): pl.pallas_call(functools.partial(chain_kernel, (tensor, dp, bulk, tiles,...  80.7 us
    pallas_call x1, Pallas kernels, error_next(): pl.pallas_call(error_kernel, out_shape=jax.ShapeDtypeStruct((head_rows, w...  21.1 us
    unnamed x14, local copies, waits for them, and re-layouts  4.02 us

profile of v1, /device:TPU:1, one launch (start us, length us, event | category | flops | bytes accessed | tf_op | source)
XLA Modules:
  0.0 110.4 jit_solution(4944876590384748962)
XLA Ops:
  0.6 0.0 copy-start
  0.6 80.7 %chain.1 = (bf16[2,512,2048]{2,1,0:T(8,128)(2,1)}, f32[64,2048]{1,0:T(8,128)}, bf16[64,4096]{1,0:T(8,128)(2,1)}, f32[64,2048]{1,0:T(8,128)}) custom-call(bf16[512,2048]{1,0:T(8,128)(2,1)} %bitcast.16, bf16[512,2048]{1,0:T(8,128)(2,1)} %bitcast.24, bf16[512,2048]{1,0:T(8,128)(2,1)} %bitcast.22, bf16[2048,4096]{1,0:T(8,128)(2,1)} %bitcast.19, f32[64,2048]{1,0:T(8,128)} %bitcast.25), custom_call_target="tpu_custom_call" | custom-call | tf_op jit(solution)/shard_map/chain/pallas_call | solution.py:358
  81.3 0.0 copy-done
  81.3 0.0 copy-start.1
  81.3 1.0 copy-done.1
  82.4 0.0 copy-start.3
  82.4 1.0 copy-done.3
  83.4 21.1 %error_next.1 = bf16[2048,4096]{1,0:T(8,128)(2,1)} custom-call(bf16[512,2048]{1,0:T(8,128)(2,1)S(1)} %bitcast.17, bf16[2,512,2048]{2,1,0:T(8,128)(2,1)} %get-tuple-element.8.g, bf16[2048,4096]{1,0:T(8,128)(2,1)} %bitcast.20, f32[64,2048]{1,0:T(8,128)S(1)} %copy-done.1, bf16[64,4096]{1,0:T(8,128)(2,1)S(1)} %copy-done.3), custom_call_target="tpu_custom_call" | custom-call | tf_op jit(solution)/shard_map/error_next/pallas_call | solution.py:423
  104.5 0.0 copy-start.4
  104.5 1.9 %constant_dynamic-slice_fusion = bf16[1,512,2048]{2,1,0:T(8,128)(2,1)S(1)} fusion(bf16[2,512,2048]{2,1,0:T(8,128)(2,1)} %get-tuple-element.8.g, s32[]{:T(128)S(6)} %select_n.4), kind=kLoop, calls=%fused_computation.2 | loop fusion | bytes 4194308 | tf_op jit(solution)/shard_map/jit(dynamic_index_in_dim)/dynamic_slice | solution.py:451
  106.4 0.3 copy-done.4
  106.7 0.0 copy-start.2
  106.7 0.0 copy-start.5
  106.7 2.1 %fusion = bf16[1,4,128,2048]{3,2,1,0:T(8,128)(2,1)} fusion(bf16[1,4,128,2048]{3,2,1,0:T(8,128)(2,1)S(1)} %bitcast.23, bf16[1,4,128,2048]{3,2,1,0:T(8,128)(2,1)S(1)} %copy-done.4), kind=kLoop, calls=%fused_computation.1 | loop fusion | flops 4194304 | bytes 6291456 | tf_op jit(solution)/shard_map/convert_element_type | solution.py:33
  108.8 0.0 copy-done.2
  108.9 0.8 copy.11
  109.6 0.0 copy-done.5
  109.6 0.8 copy.12
Async XLA Ops:
  0.6 80.7 %copy-start = (bf16[1,4,128,2048]{3,2,1,0:T(8,128)(2,1)S(1)}, bf16[1,4,128,2048]{3,2,1,0:T(8,128)(2,1)}, u32[]{:S(2)}) copy-start(bf16[1,4,128,2048]{3,2,1,0:T(8,128)(2,1)} %param.5) | copy-start | bytes 6291460
  81.3 1.0 copy-start.1
  82.4 1.0 copy-start.3
  104.5 2.2 %copy-start.4 = (bf16[1,4,128,2048]{3,2,1,0:T(8,128)(2,1)S(1)}, bf16[1,4,128,2048]{3,2,1,0:T(8,128)(2,1)}, u32[]{:S(2)}) copy-start(bf16[1,4,128,2048]{3,2,1,0:T(8,128)(2,1)} %param.7) | copy-start | bytes 6291460
  106.7 2.1 %copy-start.2 = (f32[64,2048]{1,0:T(8,128)S(1)}, f32[64,2048]{1,0:T(8,128)}, u32[]{:S(2)}) copy-start(f32[64,2048]{1,0:T(8,128)} %get-tuple-element.9.p) | copy-start | bytes 1572868
  106.7 2.9 %copy-start.5 = (f32[64,2048]{1,0:T(8,128)S(1)}, f32[64,2048]{1,0:T(8,128)}, u32[]{:S(2)}) copy-start(f32[64,2048]{1,0:T(8,128)} %get-tuple-element.11) | copy-start | bytes 1572868

commit v2 on v1

--- a/solution.py
+++ b/solution.py
@@ -59,13 +59,13 @@
     s = Semaphores()
     names = {}
     for name, n in (
-        ("err", tiles), ("g_out", 1),
+        ("err", tiles),
         ("q_s", tensor), ("q_r", tensor), ("q0_s", 1), ("q0_r", 1),
         ("bulk_s", bulk), ("bulk_r", bulk), ("gx_s", 1), ("gx_r", 1),
         ("gq_s", tensor), ("gq_r", tensor), ("p_s", dp), ("p_r", dp),
         ("pg_s", dp), ("pg_r", dp), ("gram_s", tensor), ("gram_r", tensor),
         ("ap_s", tensor), ("ap_r", tensor), ("qx_s", tensor), ("qx_r", tensor),
-        ("g_s", tensor), ("g_r", tensor), ("qp_s", dp), ("qp_r", dp),
+        ("g_s", tensor * bulk), ("g_r", tensor * bulk), ("qp_s", dp), ("qp_r", dp),
         ("qg_s", dp), ("qg_r", dp), ("qf_s", tensor * dp), ("qf_r", tensor * dp),
     ):
         names[name] = s.take(n)
@@ -74,8 +74,8 @@
 
 def chain_kernel(
     dims, attn, gtop, branch, err_hbm, q_in,
-    g_out, p_out, q_out, q_own,
-    err, qg, q0, gadd, land, gbuf, gqx, gqb, eq, psend, prcv, pg, praw, gb,
+    err, grad_in, p_out, q_out, q_own,
+    at_ref, qg, q0, land, gbuf, gqx, gqb, eq, psend, prcv, pg, praw, gb,
     phl, apb, qx, qxr, qsend, qrcv, qf, sem,
 ):
     tensor, dp, bulk, tiles, names = dims
@@ -151,9 +151,10 @@
     q0_copy = remote(qg.at[t, pl.ds(0, rank)], q0, at("q0_s"), at("q0_r"), pipe=1 - section)
     gx_copy = remote(gqx, gqb.at[t], at("gx_s"), at("gx_r"), pipe=1 - section)
     piece = tokens // bulk
+    ahead = bulk // 4
 
     def bulk_copy(i):
-        rows = pl.ds(i * piece, piece)
+        rows = pl.ds(pl.multiple_of(i * piece, piece), piece)
         return remote(branch.at[rows], land.at[rows], at("bulk_s", i), at("bulk_r", i), pipe=1 - section)
 
     @pl.when(section == 0)
@@ -162,8 +163,9 @@
 
     @pl.when(section == 1)
     def _():
-        bulk_copy(0).start()
-        gadd[...] = add_round(gtop[...], branch[...])
+        for i in range(ahead):
+            bulk_copy(i).start()
+        grad_in[...] = add_round(gtop[...], branch[...])
         gqb[t] = fold(mm(qg[t], gtop[...], NT)) * scale
 
     from_tensor(qg, "q")
@@ -182,9 +184,9 @@
     @pl.when(section == 1)
     def _():
         q0_copy.wait_recv()
-        gqx[...] = mm(q0[...], gadd[...], NT) * scale
+        gqx[...] = mm(q0[...], grad_in[...], NT) * scale
         gx_copy.start()
-        for i in range(1, bulk):
+        for i in range(ahead, bulk):
             bulk_copy(i).start()
 
     @pl.when(section == 0)
@@ -202,6 +204,13 @@
         psend[j] = p_local[:, j * pw : (j + 1) * pw]
     p_copies = over_dp(lambda peer: psend.at[peer], prcv, "p")
     start(p_copies)
+
+    def transpose_tile(i, carry):
+        rows = pl.ds(pl.multiple_of(i * tile, tile), tile)
+        at_ref[rows, :] = attn[:, rows].T
+        return carry
+
+    lax.fori_loop(0, tiles, transpose_tile, 0)
     from_dp(prcv, "p")
     total = psend[r].astype(F32)
     for peer in dp_peers:
@@ -254,15 +263,31 @@
         copy.start()
         qx_copies.append(copy)
 
-    @pl.when(section == 0)
-    def _():
-        for i in range(bulk):
+    def g_copies(i):
+        rows = pl.ds(pl.multiple_of(i * piece, piece), piece)
+        return [
+            remote(gbuf.at[t, rows], gbuf.at[t, rows], at("g_s", o * bulk + i), at("g_r", t * bulk + i), tensor=peer)
+            for o, peer in enumerate(tensor_peers)
+        ]
+
+    def land_piece(i, carry):
+        rows = pl.ds(pl.multiple_of(i * piece, piece), piece)
+
+        @pl.when(section == 0)
+        def _():
             bulk_copy(i).wait_recv()
-        gbuf[t] = add_round(gtop[...], land[...])
-
-    @pl.when(section == 1)
-    def _():
-        gbuf[t] = gtop[...]
+            out_grad = add_round(gtop[rows, :], land[rows, :])
+            gbuf[t, rows, :] = out_grad
+            grad_in[rows, :] = add_round(out_grad, branch[rows, :])
+
+        @pl.when(section == 1)
+        def _():
+            gbuf[t, rows, :] = gtop[rows, :]
+
+        start(g_copies(i))
+        return carry
+
+    lax.fori_loop(0, bulk, land_piece, 0)
 
     from_tensor(apb, "ap")
     ap = apb[0]
@@ -289,8 +314,28 @@
         qsend[j] = q_local[:, j * qw : (j + 1) * qw]
     qp_copies = over_dp(lambda peer: qsend.at[peer], qrcv, "qp")
     start(qp_copies)
-    g_copies = over_tensor(gbuf.at[t], gbuf, "g")
-    start(g_copies)
+
+    def g_landed(i, carry):
+        rows = pl.ds(pl.multiple_of(i * piece, piece), piece)
+        for peer in tensor_peers:
+            here = gbuf.at[peer, rows]
+            remote(here, here, at("g_s"), at("g_r", peer * bulk + i), tensor=peer).wait_recv()
+        return carry
+
+    lax.fori_loop(0, bulk, g_landed, 0)
+
+    def matrix_tile(i, carry):
+        rows = pl.ds(pl.multiple_of(i * tile, tile), tile)
+        acts = at_ref[rows, :]
+        for tt in range(tensor):
+            for c in range(features // step):
+                here = pl.ds(c * step, step)
+                there = pl.ds(tt * features + c * step, step)
+                value = mm(acts, gbuf[tt, :, here], NN) * scale + err[rows, there].astype(F32)
+                err[rows, there] = value.astype(BF16)
+        return carry
+
+    lax.fori_loop(0, tiles // 2, matrix_tile, 0)
     from_dp(qrcv, "qp")
     total = qsend[r].astype(F32)
     for peer in dp_peers:
@@ -310,9 +355,7 @@
             qf_copies.append(copy)
 
     forward(r)
-    from_tensor(gbuf, "g")
-    g_copy = pltpu.make_async_copy(gbuf, g_out, at("g_out"))
-    g_copy.start()
+    lax.fori_loop(tiles // 2, tiles, matrix_tile, 0)
     for peer in dp_peers:
         remote(qf.at[t, peer], qf.at[t, peer], at("qg_s"), at("qg_r", peer), dp=peer).wait_recv()
         forward(peer)
@@ -337,9 +380,14 @@
             bulk_copy(i).wait_send()
 
     for copies in (q_copies, gq_copies, p_copies, pg_copies, gram_copies, ap_copies,
-                   qx_copies, qp_copies, g_copies, qg_copies, qf_copies):
+                   qx_copies, qp_copies, qg_copies, qf_copies):
         sent(copies)
-    g_copy.wait()
+
+    def g_sent(i, carry):
+        sent(g_copies(i))
+        return carry
+
+    lax.fori_loop(0, bulk, g_sent, 0)
 
 
 def chain(mesh, attn, gtop, branch, err, q_t):
@@ -348,7 +396,7 @@
     features = gtop.shape[1]
     rank = q_t.shape[0]
     tiles = max(1, head_rows // max(128, head_rows // 8))
-    bulk = 8
+    bulk = 16
     names, count = semaphore_map(tensor, dp, bulk, tiles)
     width = tensor * features
     pw, qw = head_rows // dp, features // dp
@@ -358,18 +406,18 @@
     return pl.pallas_call(
         functools.partial(chain_kernel, (tensor, dp, bulk, tiles, names)),
         out_shape=(
-            jax.ShapeDtypeStruct((tensor, tokens, features), BF16),
-            jax.ShapeDtypeStruct((rank, head_rows), F32),
-            jax.ShapeDtypeStruct((rank, width), BF16),
-            jax.ShapeDtypeStruct((rank, features), F32),
+            pltpu.VMEM((head_rows, width), BF16),
+            pltpu.VMEM((tokens, features), BF16),
+            pltpu.VMEM((rank, head_rows), F32),
+            pltpu.VMEM((rank, width), BF16),
+            pltpu.VMEM((rank, features), F32),
         ),
         in_specs=[vmem, vmem, vmem, anywhere, vmem],
-        out_specs=(anywhere, vmem, vmem, vmem),
+        out_specs=(vmem,) * 5,
         scratch_shapes=[
-            pltpu.VMEM((head_rows, width), BF16),
+            pltpu.VMEM((head_rows, tokens), BF16),
             pltpu.VMEM((tensor, 2 * rank, features), BF16),
             pltpu.VMEM((rank, features), BF16),
-            pltpu.VMEM((tokens, features), BF16),
             pltpu.VMEM((tokens, features), BF16),
             pltpu.VMEM((tensor, tokens, features), BF16),
             pltpu.VMEM((rank, tokens), F32),
@@ -390,54 +438,77 @@
             pltpu.SemaphoreType.DMA((count,)),
         ],
         compiler_params=pltpu.CompilerParams(
-            collective_id=0, has_side_effects=True, vmem_limit_bytes=56 * 2**20
+            collective_id=0, has_side_effects=True, vmem_limit_bytes=30 * 2**20
         ),
         name="chain",
     )(attn, gtop, branch, err, q_t)
 
 
-def error_kernel(attn, g, err, p, q, out, pair):
-    tensor, tokens, features = g.shape
-    scale = 1.0 / tokens
-
-    @pl.when(pl.program_id(0) == 0)
-    def _():
-        pair[...] = jnp.concatenate([q[...], q[...]], axis=0)
-
-    acts = attn[...].T
-    fact = terms(p[...]).T
-    step = min(features, 512)
-    for tt in range(tensor):
-        for c in range(features // step):
+def finish_kernel(tiles, matrix, grad_in, p, q, q_own, out, grad_out, p_out, q_out, fact, pair, held, sem):
+    head_rows, width = matrix.shape
+    tile = head_rows // tiles
+    step = min(width, 512)
+    small = [
+        pltpu.make_async_copy(src, dst, sem.at[2 + i])
+        for i, (src, dst) in enumerate(((grad_in, grad_out), (p, p_out), (q_own, q_out)))
+    ]
+    for copy in small:
+        copy.start()
+    pair[...] = jnp.concatenate([q[...], q[...]], axis=0)
+    fact[...] = terms(p[...]).T
+
+    def out_copy(i, slot):
+        rows = pl.ds(pl.multiple_of(i * tile, tile), tile)
+        return pltpu.make_async_copy(held.at[slot], out.at[rows], sem.at[slot])
+
+    def row_tile(i, carry):
+        slot = lax.rem(i, 2)
+        rows = pl.ds(pl.multiple_of(i * tile, tile), tile)
+
+        @pl.when(i >= 2)
+        def _():
+            out_copy(i - 2, slot).wait()
+
+        for c in range(width // step):
             here = slice(c * step, (c + 1) * step)
-            there = slice(tt * features + c * step, tt * features + (c + 1) * step)
-            matrix = mm(acts, g[tt, :, here], NN) * scale + err[:, there].astype(F32)
-            out[:, there] = (matrix - mm(fact, pair[:, there], NN)).astype(BF16)
-
-
-def error_next(attn, g, err, p, q):
-    tensor, tokens, features = g.shape
-    head_rows, width = err.shape
+            value = matrix[rows, here].astype(F32) - mm(fact[rows, :], pair[:, here], NN)
+            held[slot, :, here] = value.astype(BF16)
+        out_copy(i, slot).start()
+        return carry
+
+    lax.fori_loop(0, tiles, row_tile, 0)
+    for i in range(max(0, tiles - 2), tiles):
+        out_copy(i, i % 2).wait()
+    for copy in small:
+        copy.wait()
+
+
+def finish(matrix, grad_in, p, q, q_own):
+    head_rows, width = matrix.shape
     rank = p.shape[0]
-    tile = max(128, head_rows // 8)
+    tile = max(128, head_rows // 16)
+    vmem = pl.BlockSpec(memory_space=pltpu.VMEM)
+    anywhere = pl.BlockSpec(memory_space=pl.ANY)
+    args = [pltpu.with_memory_space_constraint(x, pltpu.VMEM) for x in (matrix, grad_in, p, q, q_own)]
     return pl.pallas_call(
-        error_kernel,
-        out_shape=jax.ShapeDtypeStruct((head_rows, width), BF16),
-        grid=(head_rows // tile,),
-        in_specs=[
-            pl.BlockSpec((tokens, tile), lambda i: (0, i)),
-            pl.BlockSpec((tensor, tokens, features), lambda i: (0, 0, 0)),
-            pl.BlockSpec((tile, width), lambda i: (i, 0)),
-            pl.BlockSpec((rank, tile), lambda i: (0, i)),
-            pl.BlockSpec((rank, width), lambda i: (0, 0)),
+        functools.partial(finish_kernel, head_rows // tile),
+        out_shape=(
+            pltpu.HBM(matrix.shape, BF16),
+            pltpu.HBM(grad_in.shape, BF16),
+            pltpu.HBM(p.shape, F32),
+            pltpu.HBM(q_own.shape, F32),
+        ),
+        in_specs=[vmem] * 5,
+        out_specs=(anywhere,) * 4,
+        scratch_shapes=[
+            pltpu.VMEM((head_rows, 2 * rank), BF16),
+            pltpu.VMEM((2 * rank, width), BF16),
+            pltpu.VMEM((2, tile, width), BF16),
+            pltpu.SemaphoreType.DMA((5,)),
         ],
-        out_specs=pl.BlockSpec((tile, width), lambda i: (i, 0)),
-        scratch_shapes=[pltpu.VMEM((2 * rank, width), BF16)],
-        compiler_params=pltpu.CompilerParams(
-            dimension_semantics=("arbitrary",), vmem_limit_bytes=48 * 2**20
-        ),
-        name="error_next",
-    )(attn, g, err, p, q)
+        compiler_params=pltpu.CompilerParams(vmem_limit_bytes=12 * 2**20),
+        name="finish",
+    )(*args)
 
 
 def on_device(mesh, attn_out, grad_top, branch_grad, error_prev, q_prev):
@@ -447,11 +518,9 @@
     gtop = grad_top.reshape(tokens, features)
     branch = branch_grad.reshape(tokens, features)
     err = error_prev[0, 0]
-    g, p, q, q_own = chain(mesh, attn, gtop, branch, err, q_prev[0].T)
-    own = lax.dynamic_index_in_dim(g, lax.axis_index("tensor"), 0, keepdims=False)
-    grad_in = add_round(own, branch).reshape(branch_grad.shape)
-    error = error_next(attn, g, err, p, q)
-    return grad_in, error[None, None], p.T[None], q_own.T[None]
+    matrix, grad_in, p, q, q_own = chain(mesh, attn, gtop, branch, err, q_prev[0].T)
+    error, grad_in, p, q_own = finish(matrix, grad_in, p, q, q_own)
+    return grad_in.reshape(branch_grad.shape), error[None, None], p.T[None], q_own.T[None]
 
 
 def solution(mesh):

time: 111 us -> 90.5 us (0.82)
  Pallas kernels: 102 us -> 87 us
  local copies, waits for them, and re-layouts: 5.89 us -> 2.63 us
  other arithmetic: 2.12 us -> 0 us
    pallas_call x1, Pallas kernels: 21.1 us -> 12.2 us  [finish(): pl.pallas_call(functools.partial(finish_kernel, head_rows // tile), out_s...]
    pallas_call x1, Pallas kernels: 80.7 us -> 74.7 us  [chain(): pl.pallas_call(functools.partial(chain_kernel, (tensor, dp, bulk, tiles,...]
    convert_element_type x1 -> x0, other arithmetic: 2.12 us -> none  [add_round(): return (a.astype(F32) + b.astype(F32)).astype(BF16)]
    dynamic_slice x1 -> x0, local copies, waits for them, and re-layouts: 1.88 us -> none  [on_device(): lax.dynamic_index_in_dim(g, lax.axis_index('tensor'), 0, keepdims=False)]
    unnamed x14 -> x4, local copies, waits for them, and re-layouts: 4.02 us -> 2.63 us
where the time goes in v2:
time: 90.5 us; the launch traced here: 90.2 us
  Pallas kernels  87 us (96%)
  local copies, waits for them, and re-layouts  2.63 us (3%)
    pallas_call x1, Pallas kernels, chain(): pl.pallas_call(functools.partial(chain_kernel, (tensor, dp, bulk, tiles,...  74.7 us
    pallas_call x1, Pallas kernels, finish(): pl.pallas_call(functools.partial(finish_kernel, head_rows // tile), out_s...  12.2 us
    unnamed x4, local copies, waits for them, and re-layouts  2.63 us

profile of v2, /device:TPU:1, one launch (start us, length us, event | category | flops | bytes accessed | tf_op | source)
XLA Modules:
  0.0 90.2 jit_solution(7139358909875292978)
XLA Ops:
  0.6 0.0 copy-start
  0.6 1.6 %copy-done = bf16[1,4,128,2048]{3,2,1,0:T(8,128)(2,1)S(1)} copy-done((bf16[1,4,128,2048]{3,2,1,0:T(8,128)(2,1)S(1)}, bf16[1,4,128,2048]{3,2,1,0:T(8,128)(2,1)}, u32[]{:S(2)}) %copy-start) | copy-done | bytes 2097176
  2.2 0.0 copy-start.1
  2.2 1.0 %copy-done.1 = f32[1,2048,64]{1,2,0:T(8,128)S(1)} copy-done((f32[1,2048,64]{1,2,0:T(8,128)S(1)}, f32[1,2048,64]{1,2,0:T(8,128)}, u32[]{:S(2)}) %copy-start.1) | copy-done | bytes 524312
  3.3 74.7 %chain.1 = (bf16[2048,4096]{1,0:T(8,128)(2,1)S(1)}, bf16[512,2048]{1,0:T(8,128)(2,1)S(1)}, f32[64,2048]{1,0:T(8,128)S(1)}, bf16[64,4096]{1,0:T(8,128)(2,1)S(1)}, f32[64,2048]{1,0:T(8,128)S(1)}) custom-call(bf16[512,2048]{1,0:T(8,128)(2,1)S(1)} %bitcast.15, bf16[512,2048]{1,0:T(8,128)(2,1)} %bitcast.18, bf16[512,2048]{1,0:T(8,128)(2,1)} %bitcast.19, ...), custom_call_target="tpu_custom_call" | custom-call | tf_op jit(solution)/shard_map/chain/pallas_call | solution.py:406
  78.0 12.2 %finish.1 = (bf16[2048,4096]{1,0:T(8,128)(2,1)}, bf16[512,2048]{1,0:T(8,128)(2,1)}, f32[64,2048]{1,0:T(8,128)}, f32[64,2048]{1,0:T(8,128)}) custom-call(bf16[2048,4096]{1,0:T(8,128)(2,1)S(1)} %get-tuple-element.13.matrix, bf16[512,2048]{1,0:T(8,128)(2,1)S(1)} %get-tuple-element.14.grad_in, f32[64,2048]{1,0:T(8,128)S(1)} %get-tuple-element.15.p, ...), custom_call_target="tpu_custom_call" | custom-call | tf_op jit(solution)/shard_map/finish/pallas_call | solution.py:493
Async XLA Ops:
  0.6 1.6 %copy-start = (bf16[1,4,128,2048]{3,2,1,0:T(8,128)(2,1)S(1)}, bf16[1,4,128,2048]{3,2,1,0:T(8,128)(2,1)}, u32[]{:S(2)}) copy-start(bf16[1,4,128,2048]{3,2,1,0:T(8,128)(2,1)} %param.5) | copy-start | bytes 6291460
  2.2 1.0 %copy-start.1 = (f32[1,2048,64]{1,2,0:T(8,128)S(1)}, f32[1,2048,64]{1,2,0:T(8,128)}, u32[]{:S(2)}) copy-start(f32[1,2048,64]{1,2,0:T(8,128)} %param.9) | copy-start | bytes 1572868
